TPU v7x, 32 devices: a whole 2x2x4 slice. The times are simulated.
32 devices in a mesh: member: 2 (over y), seq: 4 (over z), dp: 2 (over x), mp: 2 (over core).
Axes of the slice: x: 2, y: 2, z: 4, core: 2. Of those that a mesh axis runs over, the one named last changes fastest.
Arguments:
- mixer_in: bfloat16 [4, 512, 3072], P(('member', 'dp'), 'seq', 'mp'), parts along dimension 0, may hold values from -6 to 6
- delta_raw: bfloat16 [4, 512, 3072], P(('member', 'dp'), 'seq', 'mp'), parts along dimension 0, may hold values from -2 to 512
- delta_bias: float32 [6144], P(('member', 'mp')), parts along dimension 0, may hold values from -4 to -2
- decay_log: float32 [6144, 16], P(('member', 'mp')), parts along dimension 0, may hold values from -12 to 1
- skip_gain: float32 [6144], P(('member', 'mp')), parts along dimension 0, may hold values from 0.5 to 1.5
- state_write: bfloat16 [4, 512, 16], P(('member', 'dp'), 'seq'), parts along dimension 0, may hold values from -5 to 5
- state_read: bfloat16 [4, 512, 16], P(('member', 'dp'), 'seq'), parts along dimension 0, may hold values from -1.5 to 1.5
- mixer_grad: bfloat16 [4, 512, 3072], P(('member', 'dp'), 'seq', 'mp'), parts along dimension 0, may hold values from -6 to 6
- attn_query: bfloat16 [4, 512, 1536], P(('member', 'dp'), 'seq', 'mp'), parts along dimension 0, may hold values from -5 to 5
- attn_key: bfloat16 [4, 512, 1536], P(('member', 'dp'), 'seq', 'mp'), parts along dimension 0, may hold values from -5 to 5
- attn_value: bfloat16 [4, 512, 1536], P(('member', 'dp'), 'seq', 'mp'), parts along dimension 0, may hold values from -6 to 6
- attn_grad: bfloat16 [4, 512, 1536], P(('member', 'dp'), 'seq', 'mp'), parts along dimension 0, may hold values from -6 to 6
- document_id: int32 [4, 512], P(('member', 'dp'), 'seq'), parts along dimension 0, may hold values from 0 to 3, never falling along the last dimension, each value on 1 to 256 neighbouring positions
Outputs:
- mixer_out: bfloat16 [4, 512, 3072], P(('member', 'dp'), 'seq', 'mp'), parts along dimension 0
- input_grad: bfloat16 [4, 512, 3072], P(('member', 'dp'), 'seq', 'mp'), parts along dimension 0
- delta_grad: bfloat16 [4, 512, 3072], P(('member', 'dp'), 'seq', 'mp'), parts along dimension 0
- decay_grad: float32 [6144, 16], P(('member', 'mp')), parts along dimension 0
- skip_grad: float32 [6144], P(('member', 'mp')), parts along dimension 0
- bias_grad: float32 [6144], P(('member', 'mp')), parts along dimension 0
- attn_out: bfloat16 [4, 512, 1536], P(('member', 'dp'), 'seq', 'mp'), parts along dimension 0
- query_grad: bfloat16 [4, 512, 1536], P(('member', 'dp'), 'seq', 'mp'), parts along dimension 0
- key_grad: bfloat16 [4, 512, 1536], P(('member', 'dp'), 'seq', 'mp'), parts along dimension 0
- value_grad: bfloat16 [4, 512, 1536], P(('member', 'dp'), 'seq', 'mp'), parts along dimension 0
There are 2 independent parts, one for each index of `member`. A program takes and returns all parts, laid end to end along the dimension named above; each array names one. Nothing has to cross between parts.
Inputs may be any that keep to these rules, and one draw needn't show every extreme that they name: `document_id`: document numbers never fall along a sequence; a document covers at most 256 positions.
All inputs are finite; a program needn't handle non-finite values.
Results may differ from a plain program's by a relative error of at most 0.024.
Values may be sent and summed in bfloat16 or wider, within the bound.
A program may use at most 128 MiB of HBM per device.

v0:
```python
import math
import jax
import jax.numpy as jnp
from jax import lax
from jax.sharding import PartitionSpec as P

HD = 96
WINDOW = 128
neg_large = -1e30
unroll_steps = 8


def prefix_2(x, axis, combine, identity, reverse):
    count, position = (lax.axis_size(axis), lax.axis_index(axis))
    everything = jax.tree.map(lambda part: lax.all_gather(part, axis), x)
    start = jax.tree.map(
        lambda part, zero: jnp.broadcast_to(jnp.asarray(zero, part.dtype), part.shape), x, identity
    )

    def lap(k, before):
        at = count - 1 - k if reverse else k
        reached = at > position if reverse else at < position
        new = combine(before, jax.tree.map(lambda part: part[at], everything))
        return jax.tree.map(lambda a, b: jnp.where(reached, a, b), new, before)

    return lax.fori_loop(0, count, lap, start)


def shifted(value, axis, steps):
    count = lax.axis_size(axis)
    leading, last = (max(0, -steps), min(count, count - steps))
    return lax.ppermute(value, axis, [(source, source + steps) for source in range(leading, last)])


def compose(earlier, later):
    return (earlier[0] * later[0], later[1] + later[0] * earlier[1])


def summaries(step_size, weighted, writes, reads, grads, rate):
    prefix = jnp.cumsum(step_size, axis=0)
    total = prefix[-1]
    suffix = total[None, :] - prefix
    through = jnp.exp(rate * total[:, None])
    ending = jnp.sum(
        weighted[:, :, None] * writes[:, None, :] * jnp.exp(suffix[:, :, None] * rate[None]), axis=0
    )
    leading = jnp.sum(
        grads[:, :, None] * reads[:, None, :] * jnp.exp(prefix[:, :, None] * rate[None]), axis=0
    )
    return (through, ending, leading)


def run_forward(start, step_size, weighted, writes, rate):
    count = step_size.shape[0] // unroll_steps

    def advance(state, items):
        sizes, weights, write_rows = items
        outputs = []
        for position in range(unroll_steps):
            state = (
                jnp.exp(sizes[position][:, None] * rate) * state
                + weights[position][:, None] * write_rows[position][None, :]
            )
            outputs.append(state)
        return (state, jnp.stack(outputs))

    shaped = (
        step_size.reshape(count, unroll_steps, -1),
        weighted.reshape(count, unroll_steps, -1),
        writes.reshape(count, unroll_steps, -1),
    )
    _, states = lax.scan(advance, start, shaped)
    return states.reshape((count * unroll_steps,) + start.shape)


def run_backward(start, step_size, inputs, grads, writes, reads, previous, rate, skip_gain):
    count = step_size.shape[0] // unroll_steps
    channels = step_size.shape[1]

    def retreat(carry, items):
        back, accum = carry
        sizes, values, outs, write_rows, read_rows, prior = items
        input_list = []
        step_list = []
        for position in reversed(range(unroll_steps)):
            decay = jnp.exp(sizes[position][:, None] * rate)
            adjoint = read_rows[position][None, :] * outs[position][:, None] + back
            through_write = jnp.sum(adjoint * write_rows[position][None, :], axis=1)
            input_list.append(through_write * sizes[position] + skip_gain * outs[position])
            tail = adjoint * prior[position] * decay
            step_list.append(values[position] * through_write + jnp.sum(tail * rate, axis=1))
            accum = accum + tail * sizes[position][:, None]
            back = decay * adjoint
        return ((back, accum), (jnp.stack(input_list[::-1]), jnp.stack(step_list[::-1])))

    shaped = (
        step_size.reshape(count, unroll_steps, -1),
        inputs.reshape(count, unroll_steps, -1),
        grads.reshape(count, unroll_steps, -1),
        writes.reshape(count, unroll_steps, -1),
        reads.reshape(count, unroll_steps, -1),
        previous.reshape((count, unroll_steps) + start.shape),
    )
    (_, accum), (input_grad, step_grad) = lax.scan(
        retreat, (start, jnp.zeros_like(start)), shaped, reverse=True
    )
    return (input_grad.reshape(-1, channels), step_grad.reshape(-1, channels), accum)


def body(
    mixer_in,
    delta_raw,
    delta_bias,
    decay_log,
    skip_gain,
    state_write,
    state_read,
    mixer_grad,
    attn_query,
    attn_key,
    attn_value,
    attn_grad,
    document_id,
):
    inputs = mixer_in[0].astype(jnp.float32)
    raws = delta_raw[0].astype(jnp.float32)
    grads = mixer_grad[0].astype(jnp.float32)
    writes = state_write[0].astype(jnp.float32)
    reads = state_read[0].astype(jnp.float32)
    rate = -jnp.exp(decay_log)
    step_size = jax.nn.softplus(raws + delta_bias[None, :])
    weighted = step_size * inputs
    through, ending, leading = summaries(step_size, weighted, writes, reads, grads, rate)
    zeros = jnp.zeros_like(through)
    ones = jnp.ones_like(through)
    forward_pair = prefix_2((through, ending), "seq", compose, (ones, zeros), False)
    backward_pair = prefix_2((through, leading), "seq", compose, (ones, zeros), True)
    state_start = forward_pair[1]
    adjoint_start = backward_pair[1]
    states = run_forward(state_start, step_size, weighted, writes, rate)
    mixed = jnp.sum(states * reads[:, None, :], axis=2) + skip_gain[None, :] * inputs
    previous = jnp.concatenate([state_start[None], states[:-1]], axis=0)
    input_grad, step_grad, decay_part = run_backward(
        adjoint_start, step_size, inputs, grads, writes, reads, previous, rate, skip_gain
    )
    raw_grad = step_grad * jax.nn.sigmoid(raws + delta_bias[None, :])
    sums = lax.psum(
        (decay_part * rate, jnp.sum(grads * inputs, axis=0), jnp.sum(raw_grad, axis=0)),
        ("seq", "dp"),
    )
    grad_scale = 1.0 / math.sqrt(inputs.shape[0] * lax.axis_size("seq") * lax.axis_size("dp"))
    query = attn_query[0]
    key_now = attn_key[0]
    value_now = attn_value[0]
    out_grad = attn_grad[0]
    length = query.shape[0]
    width = query.shape[1]
    heads = width // HD
    doc_now = (document_id[0] + 1).astype(jnp.bfloat16)
    key_before, value_before, doc_before = shifted((key_now, value_now, doc_now), "seq", 1)
    key_all = jnp.concatenate([key_before, key_now], axis=0).reshape(2 * length, heads, HD)
    value_all = jnp.concatenate([value_before, value_now], axis=0).reshape(2 * length, heads, HD)
    doc_all = jnp.concatenate([doc_before, doc_now], axis=0)
    query_heads = query.reshape(length, heads, HD)
    grad_heads = out_grad.reshape(length, heads, HD)
    offset = jnp.arange(length)[:, None] + length - jnp.arange(2 * length)[None, :]
    allowed = (offset >= 0) & (offset < WINDOW) & (doc_all[None, :] == doc_now[:, None])
    scale = 1.0 / math.sqrt(HD)
    scores = (
        jnp.einsum("qhd,khd->hqk", query_heads, key_all, preferred_element_type=jnp.float32) * scale
    )
    scores = jnp.where(allowed[None], scores, neg_large)
    top = jnp.max(scores, axis=2)
    log_total = top + jnp.log(jnp.sum(jnp.exp(scores - top[:, :, None]), axis=2))
    probs = jnp.exp(scores - log_total[:, :, None])
    probs_low = probs.astype(jnp.bfloat16)
    attended = jnp.einsum(
        "hqk,khd->qhd", probs_low, value_all, preferred_element_type=jnp.float32
    ).astype(jnp.bfloat16)
    row_term = jnp.einsum("qhd,qhd->hq", grad_heads, attended, preferred_element_type=jnp.float32)
    value_score = jnp.einsum(
        "qhd,khd->hqk", grad_heads, value_all, preferred_element_type=jnp.float32
    )
    score_grad = (probs * (value_score - row_term[:, :, None])).astype(jnp.bfloat16)
    query_grad = (
        jnp.einsum("hqk,khd->qhd", score_grad, key_all, preferred_element_type=jnp.float32) * scale
    ).astype(jnp.bfloat16)
    own_key = (
        jnp.einsum(
            "hqk,qhd->khd",
            score_grad[:, :, length:],
            query_heads,
            preferred_element_type=jnp.float32,
        )
        * scale
    )
    own_value = jnp.einsum(
        "hqk,qhd->khd", probs_low[:, :, length:], grad_heads, preferred_element_type=jnp.float32
    )
    next_query, next_grad, next_doc = shifted((query, out_grad, doc_now), "seq", -1)
    next_total, next_term = shifted((log_total, row_term), "seq", -1)
    next_query_heads = next_query.reshape(length, heads, HD)
    next_grad_heads = next_grad.reshape(length, heads, HD)
    key_heads = key_now.reshape(length, heads, HD)
    value_heads = value_now.reshape(length, heads, HD)
    next_offset = jnp.arange(length)[:, None] + length - jnp.arange(length)[None, :]
    next_allowed = (next_offset < WINDOW) & (doc_now[None, :] == next_doc[:, None])
    next_scores = (
        jnp.einsum("qhd,khd->hqk", next_query_heads, key_heads, preferred_element_type=jnp.float32)
        * scale
    )
    next_scores = jnp.where(next_allowed[None], next_scores, neg_large)
    next_probs = jnp.exp(next_scores - next_total[:, :, None])
    next_value_score = jnp.einsum(
        "qhd,khd->hqk", next_grad_heads, value_heads, preferred_element_type=jnp.float32
    )
    next_score_grad = (next_probs * (next_value_score - next_term[:, :, None])).astype(jnp.bfloat16)
    key_total = (
        own_key
        + jnp.einsum(
            "hqk,qhd->khd", next_score_grad, next_query_heads, preferred_element_type=jnp.float32
        )
        * scale
    )
    value_total = own_value + jnp.einsum(
        "hqk,qhd->khd",
        next_probs.astype(jnp.bfloat16),
        next_grad_heads,
        preferred_element_type=jnp.float32,
    )
    key_total = key_total.reshape(length, width)
    value_total = value_total.reshape(length, width)
    return (
        mixed.astype(jnp.bfloat16)[None],
        input_grad.astype(jnp.bfloat16)[None],
        raw_grad.astype(jnp.bfloat16)[None],
        sums[0] * grad_scale,
        sums[1] * grad_scale,
        sums[2] * grad_scale,
        attended.reshape(length, width)[None],
        query_grad.reshape(length, width)[None],
        key_total.astype(jnp.bfloat16)[None],
        value_total.astype(jnp.bfloat16)[None],
    )


def solution(mesh):
    return jax.shard_map(
        body,
        mesh=mesh,
        in_specs=(
            P(("member", "dp"), "seq", "mp"),
            P(("member", "dp"), "seq", "mp"),
            P(("member", "mp")),
            P(("member", "mp"), None),
            P(("member", "mp")),
            P(("member", "dp"), "seq", None),
            P(("member", "dp"), "seq", None),
            P(("member", "dp"), "seq", "mp"),
            P(("member", "dp"), "seq", "mp"),
            P(("member", "dp"), "seq", "mp"),
            P(("member", "dp"), "seq", "mp"),
            P(("member", "dp"), "seq", "mp"),
            P(("member", "dp"), "seq"),
        ),
        out_specs=(
            P(("member", "dp"), "seq", "mp"),
            P(("member", "dp"), "seq", "mp"),
            P(("member", "dp"), "seq", "mp"),
            P(("member", "mp"), None),
            P(("member", "mp")),
            P(("member", "mp")),
            P(("member", "dp"), "seq", "mp"),
            P(("member", "dp"), "seq", "mp"),
            P(("member", "dp"), "seq", "mp"),
            P(("member", "dp"), "seq", "mp"),
        ),
        check_vma=False,
    )
```

profile of v0, /device:TPU:16, one launch (start us, length us, event | category | flops | bytes accessed | tf_op | source)
XLA Modules:
  0.0 438.5 jit_solution(15867463959212674364)
XLA Ops:
  8.5 3.5 collective-permute-start.1
  12.0 2.4 collective-permute-start.3
  14.3 2.7 convert_bitcast_fusion.4
  17.1 2.7 fusion.88
  19.8 1.6 fusion.133
  28.0 1.6 multiply_exponential_fusion.8
  30.3 7.0 %multiply_reduce_fusion.16 = (f32[1536,16]{0,1:T(8,128)}, f32[1536,16]{0,1:T(8,128)S(1)}) fusion(f32[128,1536]{1,0:T(8,128)S(1)} %reduce_window_sum.11, f32[128,16]{1,0:T(8,128)} %copy.78, f32[128,1536]{1,0:T(8,128)} %get-tuple-element.855, f32[1536,16]{0,1:T(8,128)S(1)} %get-tuple-element.1339, f32[128,1536]{1,0:T(8,128)S(1)} %broadcast_subtract_fusion, ...), kind=kLoop, calls=%fused_computation.226 | loop fusion | flops 25116672 | bytes 3457024 | tf_op jit(solution)/shard_map/reduce_sum | solution.py:47
  37.3 12.9 %all-gather = f32[6144,16]{0,1:T(8,128)S(1)} all-gather(f32[1536,16]{0,1:T(8,128)S(1)} %get-tuple-element.722), channel_id=2, replica_groups=mesh['member'=2,'seq'=4,'dp'=2,'mp'=2] {'seq'}, dimensions={0}, use_global_device_ids=true | all-gather | bytes 491520 | tf_op jit(solution)/shard_map/all_gather | solution.py:15
  50.5 15.7 %all-gather.1 = f32[6144,16]{0,1:T(8,128)S(1)} all-gather(f32[1536,16]{0,1:T(8,128)} %get-tuple-element.856), channel_id=3, replica_groups=mesh['member'=2,'seq'=4,'dp'=2,'mp'=2] {'seq'}, dimensions={0}, use_global_device_ids=true | all-gather | bytes 491520 | tf_op jit(solution)/shard_map/all_gather | solution.py:15
  67.0 43.8 %while.63 = (s32[]{:T(128)}, f32[1536,16]{0,1:T(8,128)S(1)}, f32[16,8,1536,16]{2,3,1,0:T(8,128)}, f32[16,8,1536]{2,1,0:T(8,128)S(1)}, f32[1536,16]{0,1:T(8,128)S...) while((s32[]{:T(128)}, f32[1536,16]{0,1:T(8,128)S(1)}, ...), condition=%wide.region_5.6_spmd, body=%wide.region_4.5_spmd.sunk | while | flops 1966088 | bytes 4661081 | solution.py:72
  110.8 14.3 %all-gather.2 = f32[6144,16]{0,1:T(8,128)S(1)} all-gather(f32[1536,16]{0,1:T(8,128)S(1)} %copy-done.11), channel_id=4, replica_groups=mesh['member'=2,'seq'=4,'dp'=2,'mp'=2] {'seq'}, dimensions={0}, use_global_device_ids=true | all-gather | bytes 491520 | tf_op jit(solution)/shard_map/all_gather | solution.py:15
  126.1 11.5 %slice.665 = f32[127,1536,16]{1,2,0:T(8,128)} slice(f32[128,1536,16]{1,2,0:T(8,128)} %bitcast.504), slice={[0:127], [0:1536], [0:16]} | slice | bytes 24969216 | tf_op jit(solution)/shard_map/slice | solution.py:142
  137.5 11.5 %pad_maximum_fusion = f32[128,1536,16]{1,2,0:T(8,128)} fusion(f32[127,1536,16]{1,2,0:T(8,128)} %slice.665, f32[1,1536,16]{1,2,0:T(8,128)S(1)} %bitcast.506), kind=kLoop, calls=%fused_computation.225 | loop fusion | flops 3145728 | bytes 25165824 | tf_op jit(solution)/shard_map/concatenate | solution.py:142
  149.2 190.1 %while.66 = (s32[]{:T(128)}, f32[1536,16]{0,1:T(8,128)S(1)}, f32[1536,16]{0,1:T(8,128)S(1)}, bf16[16,8,1536]{2,1,0:T(8,128)(2,1)}, f32[16,8,1536]{2,1,0:T(8,128)...) while((s32[]{:T(128)}, f32[1536,16]{0,1:T(8,128)S(1)}, ...), condition=%wide.region_27.28_spmd.clone, body=%wide.region_10.27_spmd.clone.sunk | while | flops 4374539 | bytes 4418103 | solution.py:104
  154.0 1.6 fusion.169
  165.9 1.6 fusion.169
  177.7 1.6 fusion.169
  236.9 1.6 fusion.169
  260.7 1.6 fusion.169
  296.3 1.6 fusion.169
  315.2 1.7 fusion.168
  332.2 1.6 fusion.169
  340.0 5.4 %collective-permute-start.2 = (bf16[128,768]{1,0:T(8,128)(2,1)S(1)}, bf16[128,768]{1,0:T(8,128)(2,1)S(1)}, u32[]{:S(2)}, u32[]{:S(2)}) collective-permute-start(bf16[128,768]{1,0:T(8,128)(2,1)S(1)} %bitcast.530), channel_id=1, source_target_pairs={{0,4},{4,8},{8,12},{1,5},{5,9},{9,13},{2,6},{6,10},{10,14},{3,7},{... | collective-permute-start | bytes 589832 | tf_op jit(solution)/shard_map/ppermute | solution.py:32
  345.4 1.9 collective-permute-start
  347.3 4.1 collective-permute-start.4
  351.5 7.0 %multiply_reduce_fusion.17 = f32[16,8,1536]{2,1,0:T(8,128)S(1)} fusion(f32[16,8,1536,16]{2,3,1,0:T(8,128)} %get-tuple-element.531, f32[16,8,16]{2,1,0:T(8,128)S(1)} %get-tuple-element.1408), kind=kLoop, calls=%fused_computation.227 | loop fusion | flops 6094848 | bytes 13377536 | tf_op jit(solution)/shard_map/reduce_sum | solution.py:141
  360.5 30.6 %all-reduce = (f32[1536]{0:T(1024)S(1)}, f32[1536]{0:T(1024)S(1)}) all-reduce(f32[1536]{0:T(1024)S(1)} %get-tuple-element.853, f32[1536]{0:T(1024)S(1)} %fusion.118), channel_id=1, replica_groups=mesh['member'=2,'seq'=4,'dp'=2,'mp'=2] {'seq','dp'}, use_global_device_ids=true, to_apply=%region_30.31 | all-reduce | flops 3072 | bytes 24576 | tf_op jit(solution)/shard_map/psum | solution.py:147
  393.1 5.2 %collective-permute-start.6 = (bf16[128,768]{1,0:T(8,128)(2,1)S(1)}, bf16[128,768]{1,0:T(8,128)(2,1)}, u32[]{:S(2)}, u32[]{:S(2)}) collective-permute-start(bf16[128,768]{1,0:T(8,128)(2,1)S(1)} %bitcast.533), channel_id=1, source_target_pairs={{4,0},{8,4},{12,8},{5,1},{9,5},{13,9},{6,2},{10,6},{14,10},{7,3},{... | collective-permute-start | bytes 589832 | tf_op jit(solution)/shard_map/ppermute | solution.py:32
  400.5 11.9 %all-reduce.3.cloned.1.call-done = f32[1536,16]{0,1:T(8,128)} async-done(((f32[1536,16]{0,1:T(8,128)}), f32[1536,16]{0,1:T(8,128)}) %all-reduce.3.cloned.1.call-update) | async-done | bytes 98320 | tf_op jit(solution)/shard_map/psum | solution.py:147
  414.7 2.7 collective-permute-start.5
  418.7 3.1 collective-permute-start.7
  425.4 1.7 copy.93
  (562 shorter events, 249.6 us)
Async XLA Ops:
  7.2 405.2 %all-reduce.3.cloned.1.call-start = ((), (), s32[]{:S(2)}) async-start(), calls=%async_computation | async-start | bytes 196608 | tf_op jit(solution)/shard_map/psum | solution.py:147
  8.5 384.6 %collective-permute-start.1 = (bf16[128]{0:T(256)(128)(2,1)}, bf16[128]{0:T(256)(128)(2,1)}, u32[]{:S(2)}, u32[]{:S(2)}) collective-permute-start(bf16[128]{0:T(256)(128)(2,1)} %convert_bitcast_fusion.9), channel_id=1, source_target_pairs={{0,4},{4,8},{8,12},{1,5},{5,9},{9,13},{2,6},{6,10},{10,14},{3,7},{... | collective-permute-start | bytes 776 | tf_op jit(solution)/shard_map/ppermute | solution.py:32
  12.0 387.8 %collective-permute-start.3 = (bf16[128]{0:T(256)(128)(2,1)}, bf16[128]{0:T(256)(128)(2,1)}, u32[]{:S(2)}, u32[]{:S(2)}) collective-permute-start(bf16[128]{0:T(256)(128)(2,1)} %convert_bitcast_fusion.9), channel_id=1, source_target_pairs={{4,0},{8,4},{12,8},{5,1},{9,5},{13,9},{6,2},{10,6},{14,10},{7,3},{... | collective-permute-start | bytes 776 | tf_op jit(solution)/shard_map/ppermute | solution.py:32
  66.9 43.8 %copy-start.11 = (f32[1536,16]{0,1:T(8,128)S(1)}, f32[1536,16]{0,1:T(8,128)}, u32[]{:S(2)}) copy-start(f32[1536,16]{0,1:T(8,128)} %get-tuple-element.721) | copy-start | bytes 294916
  137.5 11.6 %copy-start.3 = (f32[1,128,16]{2,1,0:T(8,128)S(1)}, f32[1,128,16]{2,1,0:T(8,128)}, u32[]{:S(2)}) copy-start(f32[1,128,16]{2,1,0:T(8,128)} %copy.77) | copy-start | bytes 24580
  137.5 11.6 %copy-start.4 = (f32[1536]{0:T(1024)S(1)}, f32[1536]{0:T(1024)}, u32[]{:S(2)}) copy-start(f32[1536]{0:T(1024)} %param.25) | copy-start | bytes 18436
  149.2 190.2 %copy-start.2 = (f32[1536,16]{0,1:T(8,128)S(1)}, f32[1536,16]{0,1:T(8,128)}, u32[]{:S(2)}) copy-start(f32[1536,16]{0,1:T(8,128)} %param.24) | copy-start | bytes 294916
  149.2 190.8 %copy-start.5 = (bf16[1,128,768]{2,1,0:T(8,128)(2,1)S(1)}, bf16[1,128,768]{2,1,0:T(8,128)(2,1)}, u32[]{:S(2)}) copy-start(bf16[1,128,768]{2,1,0:T(8,128)(2,1)} %param.30) | copy-start | bytes 589828
  149.2 196.2 %copy-start.6 = (bf16[1,128,768]{2,1,0:T(8,128)(2,1)S(1)}, bf16[1,128,768]{2,1,0:T(8,128)(2,1)}, u32[]{:S(2)}) copy-start(bf16[1,128,768]{2,1,0:T(8,128)(2,1)} %param.31) | copy-start | bytes 589828
  149.2 198.1 %copy-start.7 = (bf16[1,128,768]{2,1,0:T(8,128)(2,1)S(1)}, bf16[1,128,768]{2,1,0:T(8,128)(2,1)}, u32[]{:S(2)}) copy-start(bf16[1,128,768]{2,1,0:T(8,128)(2,1)} %param.29) | copy-start | bytes 589828
  339.3 19.2 %copy-start.1 = (bf16[1,128,1536]{2,1,0:T(8,128)(2,1)S(1)}, bf16[1,128,1536]{2,1,0:T(8,128)(2,1)}, u32[]{:S(2)}) copy-start(bf16[1,128,1536]{2,1,0:T(8,128)(2,1)} %param.22) | copy-start | bytes 1179652
  339.3 19.2 %copy-start.10 = (f32[1536]{0:T(1024)S(1)}, f32[1536]{0:T(1024)}, u32[]{:S(2)}) copy-start(f32[1536]{0:T(1024)} %param.23) | copy-start | bytes 18436
  339.3 20.4 %copy-start = (bf16[1,128,1536]{2,1,0:T(8,128)(2,1)S(1)}, bf16[1,128,1536]{2,1,0:T(8,128)(2,1)}, u32[]{:S(2)}) copy-start(bf16[1,128,1536]{2,1,0:T(8,128)(2,1)} %param.21) | copy-start | bytes 1179652
  339.3 53.6 %copy-start.8 = (bf16[1,128,768]{2,1,0:T(8,128)(2,1)S(1)}, bf16[1,128,768]{2,1,0:T(8,128)(2,1)}, u32[]{:S(2)}) copy-start(bf16[1,128,768]{2,1,0:T(8,128)(2,1)} %param.32) | copy-start | bytes 589828
  340.0 73.9 %collective-permute-start.2 = (bf16[128,768]{1,0:T(8,128)(2,1)S(1)}, bf16[128,768]{1,0:T(8,128)(2,1)S(1)}, u32[]{:S(2)}, u32[]{:S(2)}) collective-permute-start(bf16[128,768]{1,0:T(8,128)(2,1)S(1)} %bitcast.530), channel_id=1, source_target_pairs={{0,4},{4,8},{8,12},{1,5},{5,9},{9,13},{2,6},{6,10},{10,14},{3,7},{... | collective-permute-start | bytes 589832 | tf_op jit(solution)/shard_map/ppermute | solution.py:32
  345.4 72.2 %collective-permute-start = (bf16[128,768]{1,0:T(8,128)(2,1)S(1)}, bf16[128,768]{1,0:T(8,128)(2,1)S(1)}, u32[]{:S(2)}, u32[]{:S(2)}) collective-permute-start(bf16[128,768]{1,0:T(8,128)(2,1)S(1)} %bitcast.531), channel_id=1, source_target_pairs={{0,4},{4,8},{8,12},{1,5},{5,9},{9,13},{2,6},{6,10},{10,14},{3,7},{... | collective-permute-start | bytes 589832 | tf_op jit(solution)/shard_map/ppermute | solution.py:32
  347.3 75.4 %collective-permute-start.4 = (bf16[128,768]{1,0:T(8,128)(2,1)S(1)}, bf16[128,768]{1,0:T(8,128)(2,1)}, u32[]{:S(2)}, u32[]{:S(2)}) collective-permute-start(bf16[128,768]{1,0:T(8,128)(2,1)S(1)} %bitcast.532), channel_id=1, source_target_pairs={{4,0},{8,4},{12,8},{5,1},{9,5},{13,9},{6,2},{10,6},{14,10},{7,3},{... | collective-permute-start | bytes 589832 | tf_op jit(solution)/shard_map/ppermute | solution.py:32
  393.1 34.8 %collective-permute-start.6 = (bf16[128,768]{1,0:T(8,128)(2,1)S(1)}, bf16[128,768]{1,0:T(8,128)(2,1)}, u32[]{:S(2)}, u32[]{:S(2)}) collective-permute-start(bf16[128,768]{1,0:T(8,128)(2,1)S(1)} %bitcast.533), channel_id=1, source_target_pairs={{4,0},{8,4},{12,8},{5,1},{9,5},{13,9},{6,2},{10,6},{14,10},{7,3},{... | collective-permute-start | bytes 589832 | tf_op jit(solution)/shard_map/ppermute | solution.py:32
  414.1 3.5 copy-start.9
  414.7 14.3 %collective-permute-start.5 = (f32[8,128]{1,0:T(8,128)S(1)}, f32[8,128]{1,0:T(8,128)S(1)}, u32[]{:S(2)}, u32[]{:S(2)}) collective-permute-start(f32[8,128]{1,0:T(8,128)S(1)} %log_add_fusion), channel_id=1, source_target_pairs={{4,0},{8,4},{12,8},{5,1},{9,5},{13,9},{6,2},{10,6},{14,10},{7,3},{... | collective-permute-start | bytes 12296 | tf_op jit(solution)/shard_map/ppermute | solution.py:32
  418.7 10.3 %collective-permute-start.7 = (f32[8,128]{1,0:T(8,128)S(1)}, f32[8,128]{1,0:T(8,128)S(1)}, u32[]{:S(2)}, u32[]{:S(2)}) collective-permute-start(f32[8,128]{1,0:T(8,128)S(1)} %get-tuple-element.860), channel_id=1, source_target_pairs={{4,0},{8,4},{12,8},{5,1},{9,5},{13,9},{6,2},{10,6},{14,10},{7,3},{... | collective-permute-start | bytes 12296 | tf_op jit(solution)/shard_map/ppermute | solution.py:32
Sparse Core Ops, SparseCore 0:
  340.1 72.2 all-reduce.2
where the time goes:
time: 447 us; the launch traced here: 439 us
  other arithmetic  200 us (45%)
  local copies, waits for them, and re-layouts  104 us (23%)
  blocking collectives  73.6 us (16%)
  starting transfers between devices  28.2 us (6%)
  between operations  14.5 us (3%)
  waiting for transfers between devices  11.9 us (3%)
  matrix products  4.72 us (1%)
    all_gather x3, blocking collectives, prefix_2(): everything = jax.tree.map(lambda part: lax.all_gather(part, axis), x)  42.9 us
    reduce_sum x32, other arithmetic, retreat(): jnp.sum(tail * rate, axis=1)  39.1 us
    add x32, other arithmetic, retreat(): values[position] * through_write + jnp.sum(tail * rate, axis=1)  32.7 us
    psum x1, blocking collectives, body(): lax.psum((decay_part * rate, jnp.sum(grads * inputs, axis=0), jnp.sum(raw...  30.6 us
    ppermute x8, starting transfers between devices, shifted(): lax.ppermute(value, axis, [(source, source + steps) for source in range(l...  28.2 us
    add x16, other arithmetic, retreat(): accum = accum + tail * sizes[position][:, None]  25 us
    slice x16, local copies, waits for them, and re-layouts, retreat(): adjoint = read_rows[position][None, :] * outs[position][:, None] + back  24.2 us
    dynamic_slice x32, local copies, waits for them, and re-layouts, run_forward(): _, states = lax.scan(advance, start, shaped)  22.2 us
  transfers between devices with their start and end apart: 9, of which 1 were waited for; matrix products, arithmetic and copies ran while one was open for 69% of the time, Pallas kernels for 0%

commit v1 on v0

--- a/solution.py
+++ b/solution.py
@@ -145,8 +145,10 @@
     )
     raw_grad = step_grad * jax.nn.sigmoid(raws + delta_bias[None, :])
     sums = lax.psum(
-        (decay_part * rate, jnp.sum(grads * inputs, axis=0), jnp.sum(raw_grad, axis=0)),
-        ("seq", "dp"),
+        lax.psum(
+            (decay_part * rate, jnp.sum(grads * inputs, axis=0), jnp.sum(raw_grad, axis=0)), "dp"
+        ),
+        "seq",
     )
     grad_scale = 1.0 / math.sqrt(inputs.shape[0] * lax.axis_size("seq") * lax.axis_size("dp"))
     query = attn_query[0]

time: 447 us -> 452 us (1.011)
  the two profiles are of different devices: /device:TPU:16 before, /device:TPU:0 now
where the time goes in v1:
time: 452 us; the launch traced here: 444 us
  other arithmetic  200 us (44%)
  local copies, waits for them, and re-layouts  104 us (23%)
  blocking collectives  74 us (16%)
  waiting for transfers between devices  27.1 us (6%)
  starting transfers between devices  17.6 us (4%)
  between operations  14.6 us (3%)
  matrix products  4.72 us (1%)
    all_gather x3, blocking collectives, prefix_2(): everything = jax.tree.map(lambda part: lax.all_gather(part, axis), x)  45.4 us
    reduce_sum x32, other arithmetic, retreat(): jnp.sum(tail * rate, axis=1)  39.1 us
    add x32, other arithmetic, retreat(): values[position] * through_write + jnp.sum(tail * rate, axis=1)  32.7 us
    psum x1, waiting for transfers between devices, body(): lax.psum(lax.psum((decay_part * rate, jnp.sum(grads * inputs, axis=0), jn...  27 us
    add x16, other arithmetic, retreat(): accum = accum + tail * sizes[position][:, None]  25 us
    slice x16, local copies, waits for them, and re-layouts, retreat(): adjoint = read_rows[position][None, :] * outs[position][:, None] + back  24.2 us
    dynamic_slice x32, local copies, waits for them, and re-layouts, run_forward(): _, states = lax.scan(advance, start, shaped)  22.2 us
    add x16, other arithmetic, retreat(): through_write * sizes[position] + skip_gain * outs[position]  21.9 us
  transfers between devices with their start and end apart: 10, of which 1 were waited for; matrix products, arithmetic and copies ran while one was open for 69% of the time, Pallas kernels for 0%

profile of v1, /device:TPU:0, one launch (start us, length us, event | category | flops | bytes accessed | tf_op | source)
XLA Modules:
  0.0 443.5 jit_solution(8906442803298692925)
XLA Ops:
  8.5 5.5 %collective-permute-start.1 = (bf16[128]{0:T(256)(128)(2,1)}, bf16[128]{0:T(256)(128)(2,1)}, u32[]{:S(2)}, u32[]{:S(2)}) collective-permute-start(bf16[128]{0:T(256)(128)(2,1)} %convert_bitcast_fusion.9), channel_id=1, source_target_pairs={{0,4},{4,8},{8,12},{1,5},{5,9},{9,13},{2,6},{6,10},{10,14},{3,7},{... | collective-permute-start | bytes 776 | tf_op jit(solution)/shard_map/ppermute | solution.py:32
  15.2 2.7 convert_bitcast_fusion.4
  18.0 2.7 fusion.88
  20.7 1.6 fusion.133
  28.9 1.6 multiply_exponential_fusion.8
  31.2 7.0 %multiply_reduce_fusion.16 = (f32[1536,16]{0,1:T(8,128)}, f32[1536,16]{0,1:T(8,128)S(1)}) fusion(f32[128,1536]{1,0:T(8,128)S(1)} %reduce_window_sum.11, f32[128,16]{1,0:T(8,128)} %copy.78, f32[128,1536]{1,0:T(8,128)} %get-tuple-element.857, f32[1536,16]{0,1:T(8,128)S(1)} %get-tuple-element.1341, f32[128,1536]{1,0:T(8,128)S(1)} %broadcast_subtract_fusion, ...), kind=kLoop, calls=%fused_computation.226 | loop fusion | flops 25116672 | bytes 3457024 | tf_op jit(solution)/shard_map/reduce_sum | solution.py:47
  38.2 15.5 %all-gather = f32[6144,16]{0,1:T(8,128)S(1)} all-gather(f32[1536,16]{0,1:T(8,128)S(1)} %get-tuple-element.722), channel_id=2, replica_groups=mesh['member'=2,'seq'=4,'dp'=2,'mp'=2] {'seq'}, dimensions={0}, use_global_device_ids=true | all-gather | bytes 491520 | tf_op jit(solution)/shard_map/all_gather | solution.py:15
  54.0 15.6 %all-gather.1 = f32[6144,16]{0,1:T(8,128)S(1)} all-gather(f32[1536,16]{0,1:T(8,128)} %get-tuple-element.858), channel_id=3, replica_groups=mesh['member'=2,'seq'=4,'dp'=2,'mp'=2] {'seq'}, dimensions={0}, use_global_device_ids=true | all-gather | bytes 491520 | tf_op jit(solution)/shard_map/all_gather | solution.py:15
  70.3 43.8 %while.63 = (s32[]{:T(128)}, f32[1536,16]{0,1:T(8,128)S(1)}, f32[16,8,1536,16]{2,3,1,0:T(8,128)}, f32[16,8,1536]{2,1,0:T(8,128)S(1)}, f32[1536,16]{0,1:T(8,128)S...) while((s32[]{:T(128)}, f32[1536,16]{0,1:T(8,128)S(1)}, ...), condition=%wide.region_5.6_spmd, body=%wide.region_4.5_spmd.sunk | while | flops 1966088 | bytes 4661081 | solution.py:72
  114.1 14.3 %all-gather.2 = f32[6144,16]{0,1:T(8,128)S(1)} all-gather(f32[1536,16]{0,1:T(8,128)S(1)} %copy-done.11), channel_id=4, replica_groups=mesh['member'=2,'seq'=4,'dp'=2,'mp'=2] {'seq'}, dimensions={0}, use_global_device_ids=true | all-gather | bytes 491520 | tf_op jit(solution)/shard_map/all_gather | solution.py:15
  129.4 11.5 %slice.665 = f32[127,1536,16]{1,2,0:T(8,128)} slice(f32[128,1536,16]{1,2,0:T(8,128)} %bitcast.504), slice={[0:127], [0:1536], [0:16]} | slice | bytes 24969216 | tf_op jit(solution)/shard_map/slice | solution.py:142
  140.9 11.5 %pad_maximum_fusion = f32[128,1536,16]{1,2,0:T(8,128)} fusion(f32[127,1536,16]{1,2,0:T(8,128)} %slice.665, f32[1,1536,16]{1,2,0:T(8,128)S(1)} %bitcast.506), kind=kLoop, calls=%fused_computation.225 | loop fusion | flops 3145728 | bytes 25165824 | tf_op jit(solution)/shard_map/concatenate | solution.py:142
  152.6 190.1 %while.66 = (s32[]{:T(128)}, f32[1536,16]{0,1:T(8,128)S(1)}, f32[1536,16]{0,1:T(8,128)S(1)}, bf16[16,8,1536]{2,1,0:T(8,128)(2,1)}, f32[16,8,1536]{2,1,0:T(8,128)...) while((s32[]{:T(128)}, f32[1536,16]{0,1:T(8,128)S(1)}, ...), condition=%wide.region_27.28_spmd.clone, body=%wide.region_10.27_spmd.clone.sunk | while | flops 4374539 | bytes 4418103 | solution.py:104
  157.4 1.6 fusion.169
  169.2 1.6 fusion.169
  181.1 1.6 fusion.169
  192.9 1.6 fusion.169
  204.8 1.6 fusion.169
  216.6 1.6 fusion.169
  228.5 1.6 fusion.169
  240.3 1.6 fusion.169
  252.2 1.6 fusion.169
  264.0 1.6 fusion.169
  318.5 1.7 fusion.168
  323.5 1.6 fusion.169
  343.4 3.6 collective-permute-start.2
  347.0 1.9 collective-permute-start
  350.5 7.0 %multiply_reduce_fusion.17 = f32[16,8,1536]{2,1,0:T(8,128)S(1)} fusion(f32[16,8,1536,16]{2,3,1,0:T(8,128)} %get-tuple-element.531, f32[16,8,16]{2,1,0:T(8,128)S(1)} %get-tuple-element.1411), kind=kLoop, calls=%fused_computation.227 | loop fusion | flops 6094848 | bytes 13377536 | tf_op jit(solution)/shard_map/reduce_sum | solution.py:141
  359.5 8.1 %all-reduce.1 = (f32[1536]{0:T(1024)S(1)}, f32[1536]{0:T(1024)S(1)}) all-reduce(f32[1536]{0:T(1024)S(1)} %get-tuple-element.855, f32[1536]{0:T(1024)S(1)} %fusion.118), channel_id=1, replica_groups=mesh['member'=2,'seq'=4,'dp'=2,'mp'=2] {'dp'}, use_global_device_ids=true, to_apply=%region_31.32 | all-reduce | flops 3072 | bytes 24576 | tf_op jit(solution)/shard_map/psum | solution.py:148
  367.6 20.5 %all-reduce = (f32[1536]{0:T(1024)S(1)}, f32[1536]{0:T(1024)S(1)}) all-reduce(f32[1536]{0:T(1024)S(1)} %get-tuple-element.785, f32[1536]{0:T(1024)S(1)} %get-tuple-element.786), channel_id=1, replica_groups=mesh['member'=2,'seq'=4,'dp'=2,'mp'=2] {'seq'}, use_global_device_ids=true, to_apply=%region_32.33 | all-reduce | flops 3072 | bytes 24576 | tf_op jit(solution)/shard_map/psum | solution.py:147
  400.6 27.0 %all-reduce.7.cloned.1.call-done = f32[1536,16]{0,1:T(8,128)} async-done(((f32[1536,16]{0,1:T(8,128)}), f32[1536,16]{0,1:T(8,128)}) %all-reduce.7.cloned.1.call-update) | async-done | bytes 98320 | tf_op jit(solution)/shard_map/psum | solution.py:147
  430.3 1.7 copy.93
  (566 shorter events, 250.1 us)
Async XLA Ops:
  7.2 386.4 %all-reduce.5.cloned.1.call-start = ((), (), s32[]{:S(2)}) async-start(), calls=%async_computation | async-start | bytes 196608 | tf_op jit(solution)/shard_map/psum | solution.py:148
  8.5 381.5 %collective-permute-start.1 = (bf16[128]{0:T(256)(128)(2,1)}, bf16[128]{0:T(256)(128)(2,1)}, u32[]{:S(2)}, u32[]{:S(2)}) collective-permute-start(bf16[128]{0:T(256)(128)(2,1)} %convert_bitcast_fusion.9), channel_id=1, source_target_pairs={{0,4},{4,8},{8,12},{1,5},{5,9},{9,13},{2,6},{6,10},{10,14},{3,7},{... | collective-permute-start | bytes 776 | tf_op jit(solution)/shard_map/ppermute | solution.py:32
  13.9 378.8 %collective-permute-start.3 = (bf16[128]{0:T(256)(128)(2,1)}, bf16[128]{0:T(256)(128)(2,1)}, u32[]{:S(2)}, u32[]{:S(2)}) collective-permute-start(bf16[128]{0:T(256)(128)(2,1)} %convert_bitcast_fusion.9), channel_id=1, source_target_pairs={{4,0},{8,4},{12,8},{5,1},{9,5},{13,9},{6,2},{10,6},{14,10},{7,3},{... | collective-permute-start | bytes 776 | tf_op jit(solution)/shard_map/ppermute | solution.py:32
  70.3 43.8 %copy-start.11 = (f32[1536,16]{0,1:T(8,128)S(1)}, f32[1536,16]{0,1:T(8,128)}, u32[]{:S(2)}) copy-start(f32[1536,16]{0,1:T(8,128)} %get-tuple-element.721) | copy-start | bytes 294916
  140.9 11.6 %copy-start.3 = (f32[1,128,16]{2,1,0:T(8,128)S(1)}, f32[1,128,16]{2,1,0:T(8,128)}, u32[]{:S(2)}) copy-start(f32[1,128,16]{2,1,0:T(8,128)} %copy.77) | copy-start | bytes 24580
  140.9 11.6 %copy-start.4 = (f32[1536]{0:T(1024)S(1)}, f32[1536]{0:T(1024)}, u32[]{:S(2)}) copy-start(f32[1536]{0:T(1024)} %param.25) | copy-start | bytes 18436
  152.5 190.2 %copy-start.2 = (f32[1536,16]{0,1:T(8,128)S(1)}, f32[1536,16]{0,1:T(8,128)}, u32[]{:S(2)}) copy-start(f32[1536,16]{0,1:T(8,128)} %param.24) | copy-start | bytes 294916
  152.5 190.9 %copy-start.5 = (bf16[1,128,768]{2,1,0:T(8,128)(2,1)S(1)}, bf16[1,128,768]{2,1,0:T(8,128)(2,1)}, u32[]{:S(2)}) copy-start(bf16[1,128,768]{2,1,0:T(8,128)(2,1)} %param.30) | copy-start | bytes 589828
  152.6 194.5 %copy-start.6 = (bf16[1,128,768]{2,1,0:T(8,128)(2,1)S(1)}, bf16[1,128,768]{2,1,0:T(8,128)(2,1)}, u32[]{:S(2)}) copy-start(bf16[1,128,768]{2,1,0:T(8,128)(2,1)} %param.31) | copy-start | bytes 589828
  152.6 196.4 %copy-start.7 = (bf16[1,128,768]{2,1,0:T(8,128)(2,1)S(1)}, bf16[1,128,768]{2,1,0:T(8,128)(2,1)}, u32[]{:S(2)}) copy-start(bf16[1,128,768]{2,1,0:T(8,128)(2,1)} %param.29) | copy-start | bytes 589828
  342.6 14.8 %copy-start.1 = (bf16[1,128,1536]{2,1,0:T(8,128)(2,1)S(1)}, bf16[1,128,1536]{2,1,0:T(8,128)(2,1)}, u32[]{:S(2)}) copy-start(bf16[1,128,1536]{2,1,0:T(8,128)(2,1)} %param.22) | copy-start | bytes 1179652
  342.6 14.8 %copy-start.10 = (f32[1536]{0:T(1024)S(1)}, f32[1536]{0:T(1024)}, u32[]{:S(2)}) copy-start(f32[1536]{0:T(1024)} %param.23) | copy-start | bytes 18436
  342.7 16.0 %copy-start = (bf16[1,128,1536]{2,1,0:T(8,128)(2,1)S(1)}, bf16[1,128,1536]{2,1,0:T(8,128)(2,1)}, u32[]{:S(2)}) copy-start(bf16[1,128,1536]{2,1,0:T(8,128)(2,1)} %param.21) | copy-start | bytes 1179652
  342.7 47.1 %copy-start.8 = (bf16[1,128,768]{2,1,0:T(8,128)(2,1)S(1)}, bf16[1,128,768]{2,1,0:T(8,128)(2,1)}, u32[]{:S(2)}) copy-start(bf16[1,128,768]{2,1,0:T(8,128)(2,1)} %param.32) | copy-start | bytes 589828
  343.4 84.2 %all-reduce.7.cloned.1.call-start = ((), (), s32[]{:S(2)}) async-start(), calls=%async_computation.1 | async-start | bytes 196608 | tf_op jit(solution)/shard_map/psum | solution.py:147
  343.4 50.2 %collective-permute-start.2 = (bf16[128,768]{1,0:T(8,128)(2,1)S(1)}, bf16[128,768]{1,0:T(8,128)(2,1)S(1)}, u32[]{:S(2)}, u32[]{:S(2)}) collective-permute-start(bf16[128,768]{1,0:T(8,128)(2,1)S(1)} %bitcast.530), channel_id=1, source_target_pairs={{0,4},{4,8},{8,12},{1,5},{5,9},{9,13},{2,6},{6,10},{10,14},{3,7},{... | collective-permute-start | bytes 589832 | tf_op jit(solution)/shard_map/ppermute | solution.py:32
  347.0 48.8 %collective-permute-start = (bf16[128,768]{1,0:T(8,128)(2,1)S(1)}, bf16[128,768]{1,0:T(8,128)(2,1)S(1)}, u32[]{:S(2)}, u32[]{:S(2)}) collective-permute-start(bf16[128,768]{1,0:T(8,128)(2,1)S(1)} %bitcast.531), channel_id=1, source_target_pairs={{0,4},{4,8},{8,12},{1,5},{5,9},{9,13},{2,6},{6,10},{10,14},{3,7},{... | collective-permute-start | bytes 589832 | tf_op jit(solution)/shard_map/ppermute | solution.py:32
  349.0 49.9 %collective-permute-start.4 = (bf16[128,768]{1,0:T(8,128)(2,1)S(1)}, bf16[128,768]{1,0:T(8,128)(2,1)}, u32[]{:S(2)}, u32[]{:S(2)}) collective-permute-start(bf16[128,768]{1,0:T(8,128)(2,1)S(1)} %bitcast.532), channel_id=1, source_target_pairs={{4,0},{8,4},{12,8},{5,1},{9,5},{13,9},{6,2},{10,6},{14,10},{7,3},{... | collective-permute-start | bytes 589832 | tf_op jit(solution)/shard_map/ppermute | solution.py:32
  390.0 42.9 %collective-permute-start.6 = (bf16[128,768]{1,0:T(8,128)(2,1)S(1)}, bf16[128,768]{1,0:T(8,128)(2,1)}, u32[]{:S(2)}, u32[]{:S(2)}) collective-permute-start(bf16[128,768]{1,0:T(8,128)(2,1)S(1)} %bitcast.533), channel_id=1, source_target_pairs={{4,0},{8,4},{12,8},{5,1},{9,5},{13,9},{6,2},{10,6},{14,10},{7,3},{... | collective-permute-start | bytes 589832 | tf_op jit(solution)/shard_map/ppermute | solution.py:32
  393.8 2.0 copy-start.9
  394.4 39.7 %collective-permute-start.5 = (f32[8,128]{1,0:T(8,128)S(1)}, f32[8,128]{1,0:T(8,128)S(1)}, u32[]{:S(2)}, u32[]{:S(2)}) collective-permute-start(f32[8,128]{1,0:T(8,128)S(1)} %log_add_fusion), channel_id=1, source_target_pairs={{4,0},{8,4},{12,8},{5,1},{9,5},{13,9},{6,2},{10,6},{14,10},{7,3},{... | collective-permute-start | bytes 12296 | tf_op jit(solution)/shard_map/ppermute | solution.py:32
  396.9 37.1 %collective-permute-start.7 = (f32[8,128]{1,0:T(8,128)S(1)}, f32[8,128]{1,0:T(8,128)S(1)}, u32[]{:S(2)}, u32[]{:S(2)}) collective-permute-start(f32[8,128]{1,0:T(8,128)S(1)} %get-tuple-element.862), channel_id=1, source_target_pairs={{4,0},{8,4},{12,8},{5,1},{9,5},{13,9},{6,2},{10,6},{14,10},{7,3},{... | collective-permute-start | bytes 12296 | tf_op jit(solution)/shard_map/ppermute | solution.py:32
Sparse Core Ops, SparseCore 0:
  343.5 22.3 all-reduce.4
  393.7 33.8 all-reduce.6
